TPU v7x, 256 devices: a whole 4x4x8 slice. The times are simulated.
256 devices in a mesh: kx: 16 (over z, x_lo), cz: 16 (over y, x_hi, core).
Axes of the slice: x: 4 (x_hi: 2, x_lo: 2; x = x_hi * 2 + x_lo), y: 4, z: 8, core: 2. Of those that a mesh axis runs over, the one named last changes fastest.
Arguments:
- field_modes: bfloat16 [512, 4, 12288], P('cz', None, 'kx'), may hold values from -6 to 6
- cotangent: bfloat16 [512, 4, 12288], P('cz', None, 'kx'), may hold values from -6 to 6
Outputs:
- mode_gradient: bfloat16 [512, 4, 12288], P('cz', None, 'kx')
All inputs are finite; a program needn't handle non-finite values.
Results may differ from a plain program's by a relative error of at most 0.009.
Values may be sent and summed in bfloat16 or wider, within the bound.
A program may use at most 128 MiB of HBM per device.

v0:
```python
import math

import jax
import jax.numpy as jnp
from jax import lax
from jax.experimental import pallas as pl
from jax.experimental.pallas import tpu as pltpu
from jax.sharding import PartitionSpec as P

NZ = 512
MZ = 768
NX = 768
Y = 16
N = 16
XB = NX // N
MESH = pl.DeviceIdType.MESH
F32 = jnp.float32
BF16 = jnp.bfloat16
NT = (((1,), (1,)), ((), ()))
TN = (((0,), (0,)), ((), ()))


def cosine_table():
    row_index = jnp.arange(MZ, dtype=jnp.int32)
    col_index = jnp.arange(NZ, dtype=jnp.int32)
    position = col_index[None, :] * (2 * row_index[:, None] + 1) % (4 * MZ)
    return jnp.cos(jnp.pi * position.astype(jnp.float32) / (2 * MZ))


def hartley_table():
    points = jnp.arange(NX, dtype=jnp.int32)
    position = points[:, None] * points[None, :] % NX
    phases = 2.0 * jnp.pi * position.astype(jnp.float32) / NX
    return ((jnp.cos(phases) + jnp.sin(phases)) / math.sqrt(NX)).astype(jnp.bfloat16)


def iota(shape, dim):
    return lax.broadcasted_iota(jnp.int32, shape, dim)


def dot(a, b, dims=(((1,), (0,)), ((), ()))):
    return lax.dot_general(a, b, dims, preferred_element_type=F32)


def kernel(
    fm_ref, ct_ref, h_hbm, st_hbm, pt_hbm, out_ref,
    h_ref, st_ref, pt_ref, send1, recv1, send2, recv2, send3, recv3, send4, recv4,
    lift_ref, tab_sem, ssem, rsem,
):
    my_kx = lax.axis_index("kx")
    my_cz = lax.axis_index("cz")
    me = {"kx": my_kx, "cz": my_cz}

    barrier = pltpu.get_barrier_semaphore()
    for axis in ("kx", "cz"):
        for d in range(1, N):
            peer = lax.rem(me[axis] + d, N)
            pl.semaphore_signal(barrier, inc=1, device_id={axis: peer}, device_id_type=MESH)
    tables = [
        pltpu.make_async_copy(src, dst, tab_sem.at[i])
        for i, (src, dst) in enumerate(((h_hbm, h_ref), (st_hbm, st_ref), (pt_hbm, pt_ref)))
    ]
    for t in tables:
        t.start()

    def exchange(stage, axis, src, dst):
        copies = []
        for d in range(1, N):
            peer = lax.rem(me[axis] + d, N)
            c = pltpu.make_async_remote_copy(
                src_ref=src.at[peer], dst_ref=dst.at[me[axis]],
                send_sem=ssem.at[stage], recv_sem=rsem.at[stage],
                device_id={axis: peer}, device_id_type=MESH,
            )
            c.start()
        dst[me[axis]] = src[me[axis]]

    def wait_recv(stage, dst):
        pltpu.make_async_copy(dst.at[pl.ds(0, N - 1)], dst.at[pl.ds(0, N - 1)], rsem.at[stage]).wait()

    def wait_send(stage, src):
        pltpu.make_async_copy(src.at[pl.ds(0, N - 1)], src.at[pl.ds(0, N - 1)], ssem.at[stage]).wait()

    r, c = iota((128, 128), 0), iota((128, 128), 1)
    perm = (c == (r % 8) * 16 + r // 8).astype(F32).astype(BF16)
    r, c = iota((512, 512), 0), iota((512, 512), 1)
    group = (c == (r % 4) * 128 + r // 4).astype(F32).astype(BF16)

    for arr, ref in enumerate((fm_ref, ct_ref)):
        parts = []
        for j in range(6):
            block = ref[:, :, 128 * j:128 * (j + 1)].reshape(128, 128)
            parts.append(dot(perm, block, NT).reshape(16, 8, 128))
        send1[arr] = jnp.concatenate(parts, axis=1).astype(BF16)
        if arr == 0:
            pl.semaphore_wait(barrier, 2 * (N - 1))
        exchange(arr, "kx", send1.at[arr], recv1.at[arr])

    for arr in range(2):
        wait_recv(arr, recv1.at[arr])
        if arr == 0:
            tables[0].wait()
        got = recv1[arr].reshape(NX, 128)
        send2[arr] = dot(h_ref[...], got).astype(BF16).reshape(N, XB, 128)
        exchange(2 + arr, "cz", send2.at[arr], recv2.at[arr])

    tables[1].wait()
    tables[2].wait()
    for arr in range(2):
        wait_recv(2 + arr, recv2.at[arr])
        rows = jnp.concatenate(
            [jnp.concatenate([recv2[arr, 4 * g + i] for i in range(4)], axis=1) for g in range(4)],
            axis=0,
        )
        rows = dot(rows, group).astype(BF16)
        rows = jnp.concatenate(
            [
                jnp.concatenate(
                    [rows[XB * g:XB * (g + 1), 128 * f:128 * (f + 1)] for g in range(4)], axis=1)
                for f in range(4)
            ],
            axis=0,
        )
        table = (st_ref, pt_ref)[arr]
        lift_ref[arr] = dot(rows, table[...]).reshape(4, XB, MZ)

    u, v, w, b = (lift_ref[0, f] for f in range(4))
    au, av, aw, ab = (lift_ref[1, f] for f in range(4))
    grad = jnp.concatenate(
        [
            (au * w).astype(BF16),
            (av * w).astype(BF16),
            (au * u + av * v + 2.0 * aw * w + ab * b).astype(BF16),
            (ab * w).astype(BF16),
        ],
        axis=0,
    )
    back = dot(grad, st_ref[...], NT).astype(BF16)
    back = jnp.concatenate(
        [
            jnp.concatenate(
                [back[XB * f:XB * (f + 1), 128 * g:128 * (g + 1)] for f in range(4)], axis=1)
            for g in range(4)
        ],
        axis=0,
    )
    back = dot(back, group, NT).astype(BF16)
    for g in range(4):
        for i in range(4):
            send3[4 * g + i] = back[XB * g:XB * (g + 1), 128 * i:128 * (i + 1)]
    exchange(4, "cz", send3, recv3)
    wait_recv(4, recv3)
    send4[...] = dot(h_ref[...], recv3[...].reshape(NX, 128)).astype(BF16).reshape(N, XB, 128)
    exchange(5, "kx", send4, recv4)
    wait_recv(5, recv4)
    got = recv4[...].astype(F32)
    for j in range(6):
        block = got[:, 8 * j:8 * (j + 1), :].reshape(128, 128).astype(BF16)
        out_ref[:, :, 128 * j:128 * (j + 1)] = dot(block, perm, TN).astype(BF16).reshape(32, 4, 128)
    for arr in range(2):
        wait_send(arr, send1.at[arr])
        wait_send(2 + arr, send2.at[arr])
    wait_send(4, send3)
    wait_send(5, send4)


def on_device(field_modes, cotangent):
    cosines = cosine_table()
    synthesis = (cosines * math.sqrt(2.0 / NZ)).astype(BF16).T
    projection = (cosines * math.sqrt(2.0 / MZ)).astype(BF16).T
    hartley = hartley_table()
    vmem = pl.BlockSpec(memory_space=pltpu.VMEM)
    hbm = pl.BlockSpec(memory_space=pl.ANY)
    one = pltpu.VMEM((N, XB, 128), BF16)
    two = pltpu.VMEM((2, N, XB, 128), BF16)
    return pl.pallas_call(
        kernel,
        out_shape=jax.ShapeDtypeStruct(field_modes.shape, BF16),
        in_specs=[vmem, vmem, hbm, hbm, hbm],
        out_specs=vmem,
        scratch_shapes=[
            pltpu.VMEM((NX, NX), BF16),
            pltpu.VMEM((NZ, MZ), BF16),
            pltpu.VMEM((NZ, MZ), BF16),
            two, two, two, two, one, one, one, one,
            pltpu.VMEM((2, 4, XB, MZ), F32),
            pltpu.SemaphoreType.DMA((3,)),
            pltpu.SemaphoreType.DMA((6,)),
            pltpu.SemaphoreType.DMA((6,)),
        ],
        compiler_params=pltpu.CompilerParams(collective_id=0, has_side_effects=True),
    )(field_modes, cotangent, hartley, synthesis, projection)


def solution(mesh):
    return jax.shard_map(
        on_device,
        mesh=mesh,
        in_specs=(P("cz", None, "kx"), P("cz", None, "kx")),
        out_specs=P("cz", None, "kx"),
        check_vma=False,
    )
```

profile of v0, /device:TPU:2, one launch (start us, length us, event | category | flops | bytes accessed | tf_op | source)
XLA Modules:
  0.0 62.2 jit_solution(15043781799477579742)
XLA Ops:
  0.0 10.6 %multiply_convert_fusion.h_hbm = bf16[768,768]{1,0:T(8,128)(2,1)} fusion(), kind=kLoop, calls=%fused_computation.4 | loop fusion | flops 7077888 | bytes 1179648 | tf_op jit(solution)/shard_map/convert_element_type | solution.py:34
  10.6 7.0 %multiply_convert_fusion.1 = (bf16[512,768]{1,0:T(8,128)(2,1)}, bf16[512,768]{1,0:T(8,128)(2,1)}) fusion(s32[768]{0:T(1024)S(1)} %multiply_add_fusion), kind=kLoop, calls=%fused_computation.12 | loop fusion | flops 5111808 | bytes 1575936 | tf_op jit(solution)/shard_map/convert_element_type | solution.py:170
  17.6 42.9 %shard_map.28 = bf16[32,4,768]{2,1,0:T(4,128)(2,1)} custom-call(bf16[32,4,768]{2,1,0:T(4,128)(2,1)} %fm_ref.1, bf16[32,4,768]{2,1,0:T(4,128)(2,1)} %ct_ref.1, bf16[768,768]{1,0:T(8,128)(2,1)} %multiply_convert_fusion.h_hbm, bf16[512,768]{1,0:T(8,128)(2,1)} %get-tuple-element.6.st_hbm, bf16[512,768]{1,0:T(8,128)(2,1)} %get-tuple-element.5.pt_hbm), custom_call_target="tpu_custom_call" | custom-call | tf_op jit(solution)/shard_map/pallas_call | solution.py:176
  60.6 1.7 %copy.4 = bf16[32,4,768]{2,1,0:T(4,128)(2,1)} copy(bf16[32,4,768]{2,1,0:T(4,128)(2,1)} %shard_map.28) | data formatting | bytes 393216
  (1 shorter events, 0.0 us)
where the time goes:
time: 62.9 us; the launch traced here: 62.2 us
  Pallas kernels  42.9 us (68%)
  other arithmetic  17.6 us (28%)
  local copies, waits for them, and re-layouts  1.67 us (3%)
    pallas_call x1, Pallas kernels, on_device(): pl.pallas_call(kernel, out_shape=jax.ShapeDtypeStruct(field_modes.shape,...  42.9 us
    convert_element_type x1, other arithmetic, hartley_table(): ((jnp.cos(phases) + jnp.sin(phases)) / math.sqrt(NX)).astype(jnp.bfloat16)  10.6 us
    convert_element_type x1, other arithmetic, on_device(): projection = (cosines * math.sqrt(2.0 / MZ)).astype(BF16).T  7.01 us
    unnamed x1, local copies, waits for them, and re-layouts  1.67 us

commit v1 on v0

--- a/solution.py
+++ b/solution.py
@@ -2,6 +2,7 @@
 
 import jax
 import jax.numpy as jnp
+import numpy as np
 from jax import lax
 from jax.experimental import pallas as pl
 from jax.experimental.pallas import tpu as pltpu
@@ -21,17 +22,17 @@
 
 
 def cosine_table():
-    row_index = jnp.arange(MZ, dtype=jnp.int32)
-    col_index = jnp.arange(NZ, dtype=jnp.int32)
+    row_index = np.arange(MZ, dtype=np.int32)
+    col_index = np.arange(NZ, dtype=np.int32)
     position = col_index[None, :] * (2 * row_index[:, None] + 1) % (4 * MZ)
-    return jnp.cos(jnp.pi * position.astype(jnp.float32) / (2 * MZ))
+    return np.cos(np.pi * position / (2 * MZ)).astype(np.float32)
 
 
 def hartley_table():
-    points = jnp.arange(NX, dtype=jnp.int32)
+    points = np.arange(NX, dtype=np.int32)
     position = points[:, None] * points[None, :] % NX
-    phases = 2.0 * jnp.pi * position.astype(jnp.float32) / NX
-    return ((jnp.cos(phases) + jnp.sin(phases)) / math.sqrt(NX)).astype(jnp.bfloat16)
+    phases = 2.0 * np.pi * position / NX
+    return ((np.cos(phases) + np.sin(phases)) / math.sqrt(NX)).astype(BF16)
 
 
 def iota(shape, dim):
@@ -166,9 +167,9 @@
 
 def on_device(field_modes, cotangent):
     cosines = cosine_table()
-    synthesis = (cosines * math.sqrt(2.0 / NZ)).astype(BF16).T
-    projection = (cosines * math.sqrt(2.0 / MZ)).astype(BF16).T
-    hartley = hartley_table()
+    synthesis = jnp.asarray((cosines * math.sqrt(2.0 / NZ)).astype(BF16).T)
+    projection = jnp.asarray((cosines * math.sqrt(2.0 / MZ)).astype(BF16).T)
+    hartley = jnp.asarray(hartley_table())
     vmem = pl.BlockSpec(memory_space=pltpu.VMEM)
     hbm = pl.BlockSpec(memory_space=pl.ANY)
     one = pltpu.VMEM((N, XB, 128), BF16)

time: 62.9 us -> 45.2 us (0.72)
  other arithmetic: 17.6 us -> 0 us
    convert_element_type x2 -> x0, other arithmetic: 17.6 us -> none  [the longest x1 10.6 us: hartley_table(): ((jnp.cos(phases) + jnp.sin(phases)) / math.sqrt(NX)).astype(jnp.bfloat16)]
where the time goes in v1:
time: 45.2 us; the launch traced here: 44.7 us
  Pallas kernels  43 us (95%)
  local copies, waits for them, and re-layouts  1.67 us (4%)
    pallas_call x1, Pallas kernels, on_device(): pl.pallas_call(kernel, out_shape=jax.ShapeDtypeStruct(field_modes.shape,...  43 us
    unnamed x1, local copies, waits for them, and re-layouts  1.67 us

profile of v1, /device:TPU:2, one launch (start us, length us, event | category | flops | bytes accessed | tf_op | source)
XLA Modules:
  0.0 44.7 jit_solution(4508619789973022554)
XLA Ops:
  0.0 43.0 %shard_map.55 = bf16[32,4,768]{2,1,0:T(4,128)(2,1)} custom-call(bf16[32,4,768]{2,1,0:T(4,128)(2,1)} %fm_ref.1, bf16[32,4,768]{2,1,0:T(4,128)(2,1)} %ct_ref.1, bf16[768,768]{1,0:T(8,128)(2,1)} %constant.8.clone.h_hbm, bf16[512,768]{1,0:T(8,128)(2,1)} %constant.6.clone.st_hbm, bf16[512,768]{1,0:T(8,128)(2,1)} %constant.7.clone.pt_hbm), custom_call_target="tpu_custom_call" | custom-call | tf_op jit(solution)/shard_map/pallas_call | solution.py:177
  43.0 1.7 %copy.7 = bf16[32,4,768]{2,1,0:T(4,128)(2,1)} copy(bf16[32,4,768]{2,1,0:T(4,128)(2,1)} %shard_map.55) | data formatting | bytes 393216

commit v2 on v1

--- a/solution.py
+++ b/solution.py
@@ -44,36 +44,79 @@
 
 
 def kernel(
-    fm_ref, ct_ref, h_hbm, st_hbm, pt_hbm, out_ref,
-    h_ref, st_ref, pt_ref, send1, recv1, send2, recv2, send3, recv3, send4, recv4,
-    lift_ref, tab_sem, ssem, rsem,
+    fm_hbm, ct_hbm, h_hbm, st_hbm, pt_hbm, out_ref,
+    in_ref, h_ref, st_ref, pt_ref, send1, recv1, send2, recv2, send3, recv3, send4, recv4,
+    lift_ref, perm_ref, group_ref, in_sem, ssem, rsem, ready, known,
 ):
     my_kx = lax.axis_index("kx")
     my_cz = lax.axis_index("cz")
     me = {"kx": my_kx, "cz": my_cz}
+    level, side = my_kx // 2, my_kx % 2
+
+    def signal(sem, axis, peer):
+        pl.semaphore_signal(sem, inc=1, device_id={axis: peer}, device_id_type=MESH)
 
     barrier = pltpu.get_barrier_semaphore()
-    for axis in ("kx", "cz"):
-        for d in range(1, N):
+    partner = my_kx + 1 - 2 * side
+    core_peer = my_cz + 1 - 2 * (my_cz % 2)
+    x_peer = my_cz + 2 - 4 * (my_cz // 2 % 2)
+    y_peers = (lax.rem(my_cz + 4, N), lax.rem(my_cz + 12, N))
+    signal(barrier, "kx", partner)
+    signal(barrier, "cz", core_peer)
+    signal(barrier, "cz", x_peer)
+    for peer in y_peers:
+        signal(barrier, "cz", peer)
+    for upper in range(4, 8):
+        @pl.when(level != upper)
+        def _():
+            for c in range(2):
+                signal(barrier, "kx", 2 * upper + c)
+    loads = [
+        pltpu.make_async_copy(src, dst, in_sem.at[i])
+        for i, (src, dst) in enumerate((
+            (fm_hbm, in_ref.at[0]), (ct_hbm, in_ref.at[1]),
+            (h_hbm, h_ref), (st_hbm, st_ref), (pt_hbm, pt_ref)))
+    ]
+    for t in loads:
+        t.start()
+    r, c = iota((128, 128), 0), iota((128, 128), 1)
+    perm_ref[...] = (c == (r % 8) * 16 + r // 8).astype(F32).astype(BF16)
+    r, c = iota((512, 512), 0), iota((512, 512), 1)
+    group_ref[...] = (c == (r % 4) * 128 + r // 4).astype(F32).astype(BF16)
+    pl.semaphore_wait(barrier, jnp.where(level >= 4, 19, jnp.where(level > 0, 6, 5)))
+
+    @pl.when(level < 3)
+    def _():
+        signal(barrier, "kx", my_kx + 2)
+
+    for lower in range(4):
+        @pl.when(level > lower)
+        def _():
+            for c in range(2):
+                signal(ready.at[level], "kx", 2 * lower + c)
+    for peer in y_peers:
+        signal(known.at[0], "cz", peer)
+
+    def copy(stage, axis, src, dst, peer):
+        return pltpu.make_async_remote_copy(
+            src_ref=src.at[peer], dst_ref=dst.at[me[axis]],
+            send_sem=ssem.at[stage], recv_sem=rsem.at[stage],
+            device_id={axis: peer}, device_id_type=MESH,
+        )
+
+    def exchange(stage, axis, src, dst, first=None):
+        if first is not None:
+            @pl.when(me[axis] != first)
+            def _():
+                copy(stage, axis, src, dst, first).start()
+        for d in (8, 7, 9, 6, 10, 5, 11, 4, 12, 3, 13, 2, 14, 1, 15):
             peer = lax.rem(me[axis] + d, N)
-            pl.semaphore_signal(barrier, inc=1, device_id={axis: peer}, device_id_type=MESH)
-    tables = [
-        pltpu.make_async_copy(src, dst, tab_sem.at[i])
-        for i, (src, dst) in enumerate(((h_hbm, h_ref), (st_hbm, st_ref), (pt_hbm, pt_ref)))
-    ]
-    for t in tables:
-        t.start()
-
-    def exchange(stage, axis, src, dst):
-        copies = []
-        for d in range(1, N):
-            peer = lax.rem(me[axis] + d, N)
-            c = pltpu.make_async_remote_copy(
-                src_ref=src.at[peer], dst_ref=dst.at[me[axis]],
-                send_sem=ssem.at[stage], recv_sem=rsem.at[stage],
-                device_id={axis: peer}, device_id_type=MESH,
-            )
-            c.start()
+            if first is None:
+                copy(stage, axis, src, dst, peer).start()
+            else:
+                @pl.when(peer != first)
+                def _():
+                    copy(stage, axis, src, dst, peer).start()
         dst[me[axis]] = src[me[axis]]
 
     def wait_recv(stage, dst):
@@ -82,38 +125,68 @@
     def wait_send(stage, src):
         pltpu.make_async_copy(src.at[pl.ds(0, N - 1)], src.at[pl.ds(0, N - 1)], ssem.at[stage]).wait()
 
-    r, c = iota((128, 128), 0), iota((128, 128), 1)
-    perm = (c == (r % 8) * 16 + r // 8).astype(F32).astype(BF16)
-    r, c = iota((512, 512), 0), iota((512, 512), 1)
-    group = (c == (r % 4) * 128 + r // 4).astype(F32).astype(BF16)
-
-    for arr, ref in enumerate((fm_ref, ct_ref)):
+    def to_level(arr, dest):
+        for c in range(2):
+            copy(arr, "kx", send1.at[arr], recv1.at[arr], 2 * dest + c).start()
+
+    for arr in range(2):
+        loads[arr].wait()
         parts = []
         for j in range(6):
-            block = ref[:, :, 128 * j:128 * (j + 1)].reshape(128, 128)
-            parts.append(dot(perm, block, NT).reshape(16, 8, 128))
+            block = in_ref[arr, :, :, 128 * j:128 * (j + 1)].reshape(128, 128)
+            parts.append(dot(perm_ref[...], block, NT).reshape(16, 8, 128))
         send1[arr] = jnp.concatenate(parts, axis=1).astype(BF16)
+        for d in (4, 3, 5, 2, 6, 1, 7):
+            dest = lax.rem(level + d, 8)
+
+            @pl.when(jnp.logical_or(level >= 4, dest < level))
+            def _():
+                to_level(arr, dest)
+        copy(arr, "kx", send1.at[arr], recv1.at[arr], partner).start()
+        recv1[arr, my_kx] = send1[arr, my_kx]
+
+    for upper in range(1, 4):
+        @pl.when(level < upper)
+        def _():
+            pl.semaphore_wait(ready.at[upper], 2)
+            for arr in range(2):
+                to_level(arr, upper)
+
+    @pl.when(level < 4)
+    def _():
+        uppers = [
+            jnp.where(level == 0, a, jnp.where(level == 1, b, jnp.where(level == 2, c, d)))
+            for a, b, c, d in ((7, 7, 4, 4), (6, 4, 5, 5), (5, 6, 7, 6), (4, 5, 6, 7))
+        ]
+        for upper in uppers:
+            pl.semaphore_wait(ready.at[upper], 2)
+            to_level(0, upper)
+        for upper in uppers:
+            to_level(1, upper)
+
+    pl.semaphore_wait(known.at[0], 2)
+    signal(known.at[1], "cz", x_peer)
+    pl.semaphore_wait(known.at[1], 1)
+    signal(known.at[2], "cz", core_peer)
+    pl.semaphore_wait(known.at[2], 1)
+
+    for arr in range(2):
         if arr == 0:
-            pl.semaphore_wait(barrier, 2 * (N - 1))
-        exchange(arr, "kx", send1.at[arr], recv1.at[arr])
-
-    for arr in range(2):
+            loads[2].wait()
         wait_recv(arr, recv1.at[arr])
-        if arr == 0:
-            tables[0].wait()
         got = recv1[arr].reshape(NX, 128)
         send2[arr] = dot(h_ref[...], got).astype(BF16).reshape(N, XB, 128)
         exchange(2 + arr, "cz", send2.at[arr], recv2.at[arr])
 
-    tables[1].wait()
-    tables[2].wait()
+    loads[3].wait()
+    loads[4].wait()
     for arr in range(2):
         wait_recv(2 + arr, recv2.at[arr])
         rows = jnp.concatenate(
             [jnp.concatenate([recv2[arr, 4 * g + i] for i in range(4)], axis=1) for g in range(4)],
             axis=0,
         )
-        rows = dot(rows, group).astype(BF16)
+        rows = dot(rows, group_ref[...]).astype(BF16)
         rows = jnp.concatenate(
             [
                 jnp.concatenate(
@@ -145,24 +218,30 @@
         ],
         axis=0,
     )
-    back = dot(back, group, NT).astype(BF16)
+    back = dot(back, group_ref[...], NT).astype(BF16)
     for g in range(4):
         for i in range(4):
             send3[4 * g + i] = back[XB * g:XB * (g + 1), 128 * i:128 * (i + 1)]
     exchange(4, "cz", send3, recv3)
     wait_recv(4, recv3)
     send4[...] = dot(h_ref[...], recv3[...].reshape(NX, 128)).astype(BF16).reshape(N, XB, 128)
-    exchange(5, "kx", send4, recv4)
+    exchange(5, "kx", send4, recv4, first=0)
     wait_recv(5, recv4)
-    got = recv4[...].astype(F32)
-    for j in range(6):
-        block = got[:, 8 * j:8 * (j + 1), :].reshape(128, 128).astype(BF16)
-        out_ref[:, :, 128 * j:128 * (j + 1)] = dot(block, perm, TN).astype(BF16).reshape(32, 4, 128)
+    out_ref[...] = recv4[...]
     for arr in range(2):
         wait_send(arr, send1.at[arr])
         wait_send(2 + arr, send2.at[arr])
     wait_send(4, send3)
     wait_send(5, send4)
+
+
+def unpack(in_ref, out_ref):
+    r, c = iota((128, 128), 0), iota((128, 128), 1)
+    perm = (c == (r % 8) * 16 + r // 8).astype(F32).astype(BF16)
+    got = in_ref[...].astype(F32)
+    for j in range(6):
+        block = got[:, 8 * j:8 * (j + 1), :].reshape(128, 128).astype(BF16)
+        out_ref[:, :, 128 * j:128 * (j + 1)] = dot(block, perm, TN).astype(BF16).reshape(32, 4, 128)
 
 
 def on_device(field_modes, cotangent):
@@ -174,23 +253,34 @@
     hbm = pl.BlockSpec(memory_space=pl.ANY)
     one = pltpu.VMEM((N, XB, 128), BF16)
     two = pltpu.VMEM((2, N, XB, 128), BF16)
-    return pl.pallas_call(
+    blocks = pl.pallas_call(
         kernel,
-        out_shape=jax.ShapeDtypeStruct(field_modes.shape, BF16),
-        in_specs=[vmem, vmem, hbm, hbm, hbm],
+        out_shape=pltpu.VMEM((N, XB, 128), BF16),
+        in_specs=[hbm] * 5,
         out_specs=vmem,
         scratch_shapes=[
+            pltpu.VMEM((2,) + field_modes.shape, BF16),
             pltpu.VMEM((NX, NX), BF16),
             pltpu.VMEM((NZ, MZ), BF16),
             pltpu.VMEM((NZ, MZ), BF16),
             two, two, two, two, one, one, one, one,
             pltpu.VMEM((2, 4, XB, MZ), F32),
-            pltpu.SemaphoreType.DMA((3,)),
+            pltpu.VMEM((128, 128), BF16),
+            pltpu.VMEM((512, 512), BF16),
+            pltpu.SemaphoreType.DMA((5,)),
             pltpu.SemaphoreType.DMA((6,)),
             pltpu.SemaphoreType.DMA((6,)),
+            pltpu.SemaphoreType.REGULAR((8,)),
+            pltpu.SemaphoreType.REGULAR((3,)),
         ],
         compiler_params=pltpu.CompilerParams(collective_id=0, has_side_effects=True),
     )(field_modes, cotangent, hartley, synthesis, projection)
+    return pl.pallas_call(
+        unpack,
+        out_shape=jax.ShapeDtypeStruct(field_modes.shape, BF16),
+        in_specs=[vmem],
+        out_specs=vmem,
+    )(pltpu.with_memory_space_constraint(blocks, pltpu.VMEM))
 
 
 def solution(mesh):

time: 45.2 us -> 43.3 us (0.958)
  local copies, waits for them, and re-layouts: 1.67 us -> 0 us
    unnamed x1 -> x0, local copies, waits for them, and re-layouts: 1.67 us -> none
    pallas_call x1 -> x2, Pallas kernels: 43 us -> 43.2 us  [the longest x1 42.3 us: on_device(): pl.pallas_call(kernel, out_shape=pltpu.VMEM((N, XB, 128), BF16), in_specs...]
where the time goes in v2:
time: 43.3 us; the launch traced here: 43.2 us
  Pallas kernels  43.2 us (100%)
    pallas_call x1, Pallas kernels, on_device(): pl.pallas_call(kernel, out_shape=pltpu.VMEM((N, XB, 128), BF16), in_specs...  42.3 us
    pallas_call x1, Pallas kernels, on_device(): pl.pallas_call(unpack, out_shape=jax.ShapeDtypeStruct(field_modes.shape,...  0.93 us

profile of v2, /device:TPU:2, one launch (start us, length us, event | category | flops | bytes accessed | tf_op | source)
XLA Modules:
  0.0 43.2 jit_solution(17322919439820724043)
XLA Ops:
  0.0 42.3 %shard_map.55.in_ref = bf16[16,48,128]{2,1,0:T(8,128)(2,1)S(1)} custom-call(bf16[32,4,768]{2,1,0:T(4,128)(2,1)} %fm_hbm.1, bf16[32,4,768]{2,1,0:T(4,128)(2,1)} %ct_hbm.1, bf16[768,768]{1,0:T(8,128)(2,1)} %constant.8.clone.h_hbm, bf16[512,768]{1,0:T(8,128)(2,1)} %constant.6.clone.st_hbm, bf16[512,768]{1,0:T(8,128)(2,1)} %constant.7.clone.pt_hbm), custom_call_target="tpu_custom_call" | custom-call | tf_op jit(solution)/shard_map/pallas_call | solution.py:256
  42.3 0.9 %shard_map.56 = bf16[32,4,768]{2,1,0:T(4,128)(2,1)} custom-call(bf16[16,48,128]{2,1,0:T(8,128)(2,1)S(1)} %shard_map.55.in_ref), custom_call_target="tpu_custom_call" | custom-call | tf_op jit(solution)/shard_map/pallas_call | solution.py:278

commit v3 on v2

--- a/solution.py
+++ b/solution.py
@@ -46,7 +46,7 @@
 def kernel(
     fm_hbm, ct_hbm, h_hbm, st_hbm, pt_hbm, out_ref,
     in_ref, h_ref, st_ref, pt_ref, send1, recv1, send2, recv2, send3, recv3, send4, recv4,
-    lift_ref, perm_ref, group_ref, in_sem, ssem, rsem, ready, known,
+    lift_ref, perm_ref, group_ref, in_sem, ssem, rsem, ready, known, chain,
 ):
     my_kx = lax.axis_index("kx")
     my_cz = lax.axis_index("cz")
@@ -67,7 +67,9 @@
     for peer in y_peers:
         signal(barrier, "cz", peer)
     for upper in range(4, 8):
-        @pl.when(level != upper)
+        near = jnp.logical_or(level == upper - 1, level == upper + 1)
+
+        @pl.when(jnp.logical_or(level < 4, near))
         def _():
             for c in range(2):
                 signal(barrier, "kx", 2 * upper + c)
@@ -83,7 +85,10 @@
     perm_ref[...] = (c == (r % 8) * 16 + r // 8).astype(F32).astype(BF16)
     r, c = iota((512, 512), 0), iota((512, 512), 1)
     group_ref[...] = (c == (r % 4) * 128 + r // 4).astype(F32).astype(BF16)
-    pl.semaphore_wait(barrier, jnp.where(level >= 4, 19, jnp.where(level > 0, 6, 5)))
+    ends = jnp.logical_or(level == 4, level == 7)
+    middle = jnp.logical_or(level == 5, level == 6)
+    entered = jnp.where(ends, 15, jnp.where(middle, 17, jnp.where(level > 0, 6, 5)))
+    pl.semaphore_wait(barrier, entered)
 
     @pl.when(level < 3)
     def _():
@@ -94,6 +99,11 @@
         def _():
             for c in range(2):
                 signal(ready.at[level], "kx", 2 * lower + c)
+    @pl.when(middle)
+    def _():
+        signal(chain.at[0], "kx", my_kx + 2)
+        signal(chain.at[1], "kx", my_kx - 2)
+
     for peer in y_peers:
         signal(known.at[0], "cz", peer)
 
@@ -104,19 +114,15 @@
             device_id={axis: peer}, device_id_type=MESH,
         )
 
-    def exchange(stage, axis, src, dst, first=None):
-        if first is not None:
-            @pl.when(me[axis] != first)
-            def _():
-                copy(stage, axis, src, dst, first).start()
-        for d in (8, 7, 9, 6, 10, 5, 11, 4, 12, 3, 13, 2, 14, 1, 15):
-            peer = lax.rem(me[axis] + d, N)
-            if first is None:
-                copy(stage, axis, src, dst, peer).start()
-            else:
-                @pl.when(peer != first)
+    def exchange(stage, axis, src, dst, by_index=False):
+        if by_index:
+            for peer in range(N):
+                @pl.when(me[axis] != peer)
                 def _():
                     copy(stage, axis, src, dst, peer).start()
+        else:
+            for d in (8, 7, 9, 6, 10, 5, 11, 4, 12, 3, 13, 2, 14, 1, 15):
+                copy(stage, axis, src, dst, lax.rem(me[axis] + d, N)).start()
         dst[me[axis]] = src[me[axis]]
 
     def wait_recv(stage, dst):
@@ -129,21 +135,63 @@
         for c in range(2):
             copy(arr, "kx", send1.at[arr], recv1.at[arr], 2 * dest + c).start()
 
-    for arr in range(2):
+    def prepare(arr):
         loads[arr].wait()
         parts = []
         for j in range(6):
             block = in_ref[arr, :, :, 128 * j:128 * (j + 1)].reshape(128, 128)
             parts.append(dot(perm_ref[...], block, NT).reshape(16, 8, 128))
         send1[arr] = jnp.concatenate(parts, axis=1).astype(BF16)
+
+    def to_levels(arr, allowed):
         for d in (4, 3, 5, 2, 6, 1, 7):
             dest = lax.rem(level + d, 8)
 
-            @pl.when(jnp.logical_or(level >= 4, dest < level))
+            @pl.when(allowed(dest, d))
             def _():
                 to_level(arr, dest)
+
+    def to_partner(arr):
         copy(arr, "kx", send1.at[arr], recv1.at[arr], partner).start()
         recv1[arr, my_kx] = send1[arr, my_kx]
+
+    def lower_ones(dest, d):
+        low = jnp.logical_and(dest < 4, jnp.logical_or(level >= 4, dest < level))
+        return jnp.logical_or(low, jnp.logical_and(level >= 4, dest >= 4)) if d in (1, 7) else low
+
+    prepare(0)
+    to_levels(0, lower_ones)
+    to_partner(0)
+    prepare(1)
+
+    @pl.when(level == 5)
+    def _():
+        pl.semaphore_wait(chain.at[1], 1)
+        signal(chain.at[3], "kx", my_kx - 2)
+        to_level(0, 7)
+
+    @pl.when(level == 6)
+    def _():
+        pl.semaphore_wait(chain.at[0], 1)
+        signal(chain.at[2], "kx", my_kx + 2)
+        to_level(0, 4)
+
+    @pl.when(level == 4)
+    def _():
+        pl.semaphore_wait(chain.at[1], 1)
+        to_level(0, 6)
+        pl.semaphore_wait(chain.at[3], 1)
+        to_level(0, 7)
+
+    @pl.when(level == 7)
+    def _():
+        pl.semaphore_wait(chain.at[0], 1)
+        to_level(0, 5)
+        pl.semaphore_wait(chain.at[2], 1)
+        to_level(0, 4)
+
+    to_levels(1, lambda dest, d: jnp.logical_or(level >= 4, dest < level))
+    to_partner(1)
 
     for upper in range(1, 4):
         @pl.when(level < upper)
@@ -161,7 +209,10 @@
         for upper in uppers:
             pl.semaphore_wait(ready.at[upper], 2)
             to_level(0, upper)
-        for upper in uppers:
+        for upper in [
+            jnp.where(level == 0, a, jnp.where(level == 1, b, jnp.where(level == 2, c, d)))
+            for a, b, c, d in ((5, 6, 5, 6), (6, 5, 6, 5), (7, 7, 4, 4), (4, 4, 7, 7))
+        ]:
             to_level(1, upper)
 
     pl.semaphore_wait(known.at[0], 2)
@@ -225,7 +276,7 @@
     exchange(4, "cz", send3, recv3)
     wait_recv(4, recv3)
     send4[...] = dot(h_ref[...], recv3[...].reshape(NX, 128)).astype(BF16).reshape(N, XB, 128)
-    exchange(5, "kx", send4, recv4, first=0)
+    exchange(5, "kx", send4, recv4, by_index=True)
     wait_recv(5, recv4)
     out_ref[...] = recv4[...]
     for arr in range(2):
@@ -272,6 +323,7 @@
             pltpu.SemaphoreType.DMA((6,)),
             pltpu.SemaphoreType.REGULAR((8,)),
             pltpu.SemaphoreType.REGULAR((3,)),
+            pltpu.SemaphoreType.REGULAR((4,)),
         ],
         compiler_params=pltpu.CompilerParams(collective_id=0, has_side_effects=True),
     )(field_modes, cotangent, hartley, synthesis, projection)

time: 43.3 us -> 42.3 us (0.977); the launches traced: 43.2 us -> 41.7 us
  Pallas kernels: 43.2 us -> 41.7 us
    pallas_call x1, Pallas kernels: 42.3 us -> 40.8 us  [on_device(): pl.pallas_call(kernel, out_shape=pltpu.VMEM((N, XB, 128), BF16), in_specs...]
where the time goes in v3:
time: 42.3 us; the launch traced here: 41.7 us
  Pallas kernels  41.7 us (99%)
    pallas_call x1, Pallas kernels, on_device(): pl.pallas_call(kernel, out_shape=pltpu.VMEM((N, XB, 128), BF16), in_specs...  40.8 us
    pallas_call x1, Pallas kernels, on_device(): pl.pallas_call(unpack, out_shape=jax.ShapeDtypeStruct(field_modes.shape,...  0.93 us

profile of v3, /device:TPU:2, one launch (start us, length us, event | category | flops | bytes accessed | tf_op | source)
XLA Modules:
  0.0 41.7 jit_solution(14358383039733683384)
XLA Ops:
  0.0 40.8 %shard_map.55.in_ref = bf16[16,48,128]{2,1,0:T(8,128)(2,1)S(1)} custom-call(bf16[32,4,768]{2,1,0:T(4,128)(2,1)} %fm_hbm.1, bf16[32,4,768]{2,1,0:T(4,128)(2,1)} %ct_hbm.1, bf16[768,768]{1,0:T(8,128)(2,1)} %constant.8.clone.h_hbm, bf16[512,768]{1,0:T(8,128)(2,1)} %constant.6.clone.st_hbm, bf16[512,768]{1,0:T(8,128)(2,1)} %constant.7.clone.pt_hbm), custom_call_target="tpu_custom_call" | custom-call | tf_op jit(solution)/shard_map/pallas_call | solution.py:307
  40.8 0.9 %shard_map.56 = bf16[32,4,768]{2,1,0:T(4,128)(2,1)} custom-call(bf16[16,48,128]{2,1,0:T(8,128)(2,1)S(1)} %shard_map.55.in_ref), custom_call_target="tpu_custom_call" | custom-call | tf_op jit(solution)/shard_map/pallas_call | solution.py:330

commit v4 on v3

--- a/solution.py
+++ b/solution.py
@@ -14,6 +14,7 @@
 Y = 16
 N = 16
 XB = NX // N
+PARTS = 4
 MESH = pl.DeviceIdType.MESH
 F32 = jnp.float32
 BF16 = jnp.bfloat16
@@ -114,6 +115,12 @@
             device_id={axis: peer}, device_id_type=MESH,
         )
 
+    def flipped(index, bits):
+        for bit in (1, 2, 4, 8):
+            if bits & bit:
+                index = index + bit - 2 * bit * (index // bit % 2)
+        return index
+
     def exchange(stage, axis, src, dst, by_index=False):
         if by_index:
             for peer in range(N):
@@ -121,8 +128,12 @@
                 def _():
                     copy(stage, axis, src, dst, peer).start()
         else:
-            for d in (8, 7, 9, 6, 10, 5, 11, 4, 12, 3, 13, 2, 14, 1, 15):
-                copy(stage, axis, src, dst, lax.rem(me[axis] + d, N)).start()
+            flip = {0: me[axis]}
+            for d in range(1, N):
+                low = d & -d
+                flip[d] = flipped(flip[d - low], low)
+            for d in (10, 11, 14, 15, 6, 7, 8, 9, 2, 3, 12, 13, 4, 5, 1):
+                copy(stage, axis, src, dst, flip[d]).start()
         dst[me[axis]] = src[me[axis]]
 
     def wait_recv(stage, dst):
@@ -190,15 +201,28 @@
         pl.semaphore_wait(chain.at[2], 1)
         to_level(0, 4)
 
-    to_levels(1, lambda dest, d: jnp.logical_or(level >= 4, dest < level))
-    to_partner(1)
-
+    def rest_of_b():
+        to_levels(1, lambda dest, d: level >= 4)
+
+        @pl.when(level < 4)
+        def _():
+            for upper in range(1, 4):
+                @pl.when(level < upper)
+                def _():
+                    to_level(1, upper)
+            for upper in [
+                jnp.where(level == 0, a, jnp.where(level == 1, b, jnp.where(level == 2, c, d)))
+                for a, b, c, d in ((5, 6, 5, 6), (6, 5, 6, 5), (7, 7, 4, 4), (4, 4, 7, 7))
+            ]:
+                to_level(1, upper)
+        to_partner(1)
+
+    to_levels(1, lambda dest, d: jnp.logical_and(level < 4, dest < level))
     for upper in range(1, 4):
         @pl.when(level < upper)
         def _():
             pl.semaphore_wait(ready.at[upper], 2)
-            for arr in range(2):
-                to_level(arr, upper)
+            to_level(0, upper)
 
     @pl.when(level < 4)
     def _():
@@ -209,25 +233,32 @@
         for upper in uppers:
             pl.semaphore_wait(ready.at[upper], 2)
             to_level(0, upper)
-        for upper in [
-            jnp.where(level == 0, a, jnp.where(level == 1, b, jnp.where(level == 2, c, d)))
-            for a, b, c, d in ((5, 6, 5, 6), (6, 5, 6, 5), (7, 7, 4, 4), (4, 4, 7, 7))
-        ]:
-            to_level(1, upper)
-
+
+    @pl.when(my_cz % 2 == 0)
+    def _():
+        rest_of_b()
     pl.semaphore_wait(known.at[0], 2)
     signal(known.at[1], "cz", x_peer)
     pl.semaphore_wait(known.at[1], 1)
     signal(known.at[2], "cz", core_peer)
     pl.semaphore_wait(known.at[2], 1)
 
+    def transformed(i, got):
+        rows = NX // PARTS
+        return dot(h_ref[rows * i:rows * (i + 1)], got).astype(BF16).reshape(N // PARTS, XB, 128)
+
     for arr in range(2):
         if arr == 0:
             loads[2].wait()
         wait_recv(arr, recv1.at[arr])
         got = recv1[arr].reshape(NX, 128)
-        send2[arr] = dot(h_ref[...], got).astype(BF16).reshape(N, XB, 128)
+        for i in range(PARTS):
+            send2[arr, 8 // PARTS * 2 * i:8 // PARTS * 2 * (i + 1)] = transformed(i, got)
         exchange(2 + arr, "cz", send2.at[arr], recv2.at[arr])
+        if arr == 0:
+            @pl.when(my_cz % 2 == 1)
+            def _():
+                rest_of_b()
 
     loads[3].wait()
     loads[4].wait()
@@ -275,7 +306,9 @@
             send3[4 * g + i] = back[XB * g:XB * (g + 1), 128 * i:128 * (i + 1)]
     exchange(4, "cz", send3, recv3)
     wait_recv(4, recv3)
-    send4[...] = dot(h_ref[...], recv3[...].reshape(NX, 128)).astype(BF16).reshape(N, XB, 128)
+    got = recv3[...].reshape(NX, 128)
+    for i in range(PARTS):
+        send4[8 // PARTS * 2 * i:8 // PARTS * 2 * (i + 1)] = transformed(i, got)
     exchange(5, "kx", send4, recv4, by_index=True)
     wait_recv(5, recv4)
     out_ref[...] = recv4[...]

time: 42.3 us -> 41 us (0.969); the launches traced: 41.7 us -> 40.9 us
  Pallas kernels: 41.7 us -> 40.9 us
    pallas_call x1, Pallas kernels: 40.8 us -> 40 us  [on_device(): pl.pallas_call(kernel, out_shape=pltpu.VMEM((N, XB, 128), BF16), in_specs...]
where the time goes in v4:
time: 41 us; the launch traced here: 40.9 us
  Pallas kernels  40.9 us (100%)
    pallas_call x1, Pallas kernels, on_device(): pl.pallas_call(kernel, out_shape=pltpu.VMEM((N, XB, 128), BF16), in_specs...  40 us
    pallas_call x1, Pallas kernels, on_device(): pl.pallas_call(unpack, out_shape=jax.ShapeDtypeStruct(field_modes.shape,...  0.93 us

profile of v4, /device:TPU:2, one launch (start us, length us, event | category | flops | bytes accessed | tf_op | source)
XLA Modules:
  0.0 40.9 jit_solution(18404145110947921582)
XLA Ops:
  0.0 40.0 %shard_map.55.in_ref = bf16[16,48,128]{2,1,0:T(8,128)(2,1)S(1)} custom-call(bf16[32,4,768]{2,1,0:T(4,128)(2,1)} %fm_hbm.1, bf16[32,4,768]{2,1,0:T(4,128)(2,1)} %ct_hbm.1, bf16[768,768]{1,0:T(8,128)(2,1)} %constant.8.clone.h_hbm, bf16[512,768]{1,0:T(8,128)(2,1)} %constant.6.clone.st_hbm, bf16[512,768]{1,0:T(8,128)(2,1)} %constant.7.clone.pt_hbm), custom_call_target="tpu_custom_call" | custom-call | tf_op jit(solution)/shard_map/pallas_call | solution.py:340
  40.0 0.9 %shard_map.56 = bf16[32,4,768]{2,1,0:T(4,128)(2,1)} custom-call(bf16[16,48,128]{2,1,0:T(8,128)(2,1)S(1)} %shard_map.55.in_ref), custom_call_target="tpu_custom_call" | custom-call | tf_op jit(solution)/shard_map/pallas_call | solution.py:363

commit v5 on v4

--- a/solution.py
+++ b/solution.py
@@ -70,7 +70,7 @@
     for upper in range(4, 8):
         near = jnp.logical_or(level == upper - 1, level == upper + 1)
 
-        @pl.when(jnp.logical_or(level < 4, near))
+        @pl.when(jnp.logical_or(level < (2 if upper == 7 else 4), near))
         def _():
             for c in range(2):
                 signal(barrier, "kx", 2 * upper + c)
@@ -88,7 +88,7 @@
     group_ref[...] = (c == (r % 4) * 128 + r // 4).astype(F32).astype(BF16)
     ends = jnp.logical_or(level == 4, level == 7)
     middle = jnp.logical_or(level == 5, level == 6)
-    entered = jnp.where(ends, 15, jnp.where(middle, 17, jnp.where(level > 0, 6, 5)))
+    entered = jnp.where(ends, jnp.where(level == 7, 11, 15), jnp.where(middle, 17, jnp.where(level > 0, 6, 5)))
     pl.semaphore_wait(barrier, entered)
 
     @pl.when(level < 3)
@@ -96,7 +96,7 @@
         signal(barrier, "kx", my_kx + 2)
 
     for lower in range(4):
-        @pl.when(level > lower)
+        @pl.when(jnp.logical_and(level > lower, level < (8 if lower < 2 else 7)))
         def _():
             for c in range(2):
                 signal(ready.at[level], "kx", 2 * lower + c)
@@ -121,7 +121,11 @@
                 index = index + bit - 2 * bit * (index // bit % 2)
         return index
 
-    def exchange(stage, axis, src, dst, by_index=False):
+    def exchange(stage, axis, src, dst, by_index=False, first=()):
+        for peer in first:
+            @pl.when(me[axis] != peer)
+            def _():
+                copy(stage, axis, src, dst, peer).start()
         if by_index:
             for peer in range(N):
                 @pl.when(me[axis] != peer)
@@ -133,7 +137,12 @@
                 low = d & -d
                 flip[d] = flipped(flip[d - low], low)
             for d in (10, 11, 14, 15, 6, 7, 8, 9, 2, 3, 12, 13, 4, 5, 1):
-                copy(stage, axis, src, dst, flip[d]).start()
+                if first:
+                    @pl.when(flip[d] >= len(first))
+                    def _():
+                        copy(stage, axis, src, dst, flip[d]).start()
+                else:
+                    copy(stage, axis, src, dst, flip[d]).start()
         dst[me[axis]] = src[me[axis]]
 
     def wait_recv(stage, dst):
@@ -167,12 +176,22 @@
         recv1[arr, my_kx] = send1[arr, my_kx]
 
     def lower_ones(dest, d):
-        low = jnp.logical_and(dest < 4, jnp.logical_or(level >= 4, dest < level))
+        low = jnp.logical_and(dest < jnp.where(level == 7, 2, 4), jnp.logical_or(level >= 4, dest < level))
         return jnp.logical_or(low, jnp.logical_and(level >= 4, dest >= 4)) if d in (1, 7) else low
 
     prepare(0)
     to_levels(0, lower_ones)
     to_partner(0)
+
+    @pl.when(level == 7)
+    def _():
+        pl.semaphore_wait(chain.at[0], 1)
+        for lower in (2, 3):
+            for c in range(2):
+                signal(ready.at[7], "kx", 2 * lower + c)
+        for dest in (3, 2, 5):
+            to_level(0, dest)
+
     prepare(1)
 
     @pl.when(level == 5)
@@ -196,13 +215,12 @@
 
     @pl.when(level == 7)
     def _():
-        pl.semaphore_wait(chain.at[0], 1)
-        to_level(0, 5)
         pl.semaphore_wait(chain.at[2], 1)
         to_level(0, 4)
 
     def rest_of_b():
-        to_levels(1, lambda dest, d: level >= 4)
+        to_levels(1, lambda dest, d: dest < jnp.where(level >= 4, 4, level))
+        to_levels(1, lambda dest, d: jnp.logical_and(level >= 4, dest >= 4))
 
         @pl.when(level < 4)
         def _():
@@ -217,7 +235,6 @@
                 to_level(1, upper)
         to_partner(1)
 
-    to_levels(1, lambda dest, d: jnp.logical_and(level < 4, dest < level))
     for upper in range(1, 4):
         @pl.when(level < upper)
         def _():
@@ -242,6 +259,10 @@
     pl.semaphore_wait(known.at[1], 1)
     signal(known.at[2], "cz", core_peer)
     pl.semaphore_wait(known.at[2], 1)
+
+    @pl.when(my_cz % 2 == 1)
+    def _():
+        rest_of_b()
 
     def transformed(i, got):
         rows = NX // PARTS
@@ -255,10 +276,6 @@
         for i in range(PARTS):
             send2[arr, 8 // PARTS * 2 * i:8 // PARTS * 2 * (i + 1)] = transformed(i, got)
         exchange(2 + arr, "cz", send2.at[arr], recv2.at[arr])
-        if arr == 0:
-            @pl.when(my_cz % 2 == 1)
-            def _():
-                rest_of_b()
 
     loads[3].wait()
     loads[4].wait()
@@ -304,7 +321,7 @@
     for g in range(4):
         for i in range(4):
             send3[4 * g + i] = back[XB * g:XB * (g + 1), 128 * i:128 * (i + 1)]
-    exchange(4, "cz", send3, recv3)
+    exchange(4, "cz", send3, recv3, first=(0, 1))
     wait_recv(4, recv3)
     got = recv3[...].reshape(NX, 128)
     for i in range(PARTS):

time: 41 us -> 40.3 us (0.983)
  Pallas kernels: 40.9 us -> 40.2 us
    pallas_call x1, Pallas kernels: 40 us -> 39.3 us  [on_device(): pl.pallas_call(kernel, out_shape=pltpu.VMEM((N, XB, 128), BF16), in_specs...]
where the time goes in v5:
time: 40.3 us; the launch traced here: 40.2 us
  Pallas kernels  40.2 us (100%)
    pallas_call x1, Pallas kernels, on_device(): pl.pallas_call(kernel, out_shape=pltpu.VMEM((N, XB, 128), BF16), in_specs...  39.3 us
    pallas_call x1, Pallas kernels, on_device(): pl.pallas_call(unpack, out_shape=jax.ShapeDtypeStruct(field_modes.shape,...  0.93 us

profile of v5, /device:TPU:2, one launch (start us, length us, event | category | flops | bytes accessed | tf_op | source)
XLA Modules:
  0.0 40.2 jit_solution(16028689902024378883)
XLA Ops:
  0.0 39.3 %shard_map.55.in_ref = bf16[16,48,128]{2,1,0:T(8,128)(2,1)S(1)} custom-call(bf16[32,4,768]{2,1,0:T(4,128)(2,1)} %fm_hbm.1, bf16[32,4,768]{2,1,0:T(4,128)(2,1)} %ct_hbm.1, bf16[768,768]{1,0:T(8,128)(2,1)} %constant.8.clone.h_hbm, bf16[512,768]{1,0:T(8,128)(2,1)} %constant.6.clone.st_hbm, bf16[512,768]{1,0:T(8,128)(2,1)} %constant.7.clone.pt_hbm), custom_call_target="tpu_custom_call" | custom-call | tf_op jit(solution)/shard_map/pallas_call | solution.py:357
  39.3 0.9 %shard_map.56 = bf16[32,4,768]{2,1,0:T(4,128)(2,1)} custom-call(bf16[16,48,128]{2,1,0:T(8,128)(2,1)S(1)} %shard_map.55.in_ref), custom_call_target="tpu_custom_call" | custom-call | tf_op jit(solution)/shard_map/pallas_call | solution.py:380

commit v6 on v5

--- a/solution.py
+++ b/solution.py
@@ -128,6 +128,8 @@
                 copy(stage, axis, src, dst, peer).start()
         if by_index:
             for peer in range(N):
+                peer = lax.rem(peer + jnp.where(level < 4, 8, 0), N)
+
                 @pl.when(me[axis] != peer)
                 def _():
                     copy(stage, axis, src, dst, peer).start()
@@ -230,7 +232,7 @@
                     to_level(1, upper)
             for upper in [
                 jnp.where(level == 0, a, jnp.where(level == 1, b, jnp.where(level == 2, c, d)))
-                for a, b, c, d in ((5, 6, 5, 6), (6, 5, 6, 5), (7, 7, 4, 4), (4, 4, 7, 7))
+                for a, b, c, d in ((4, 4, 7, 7), (5, 5, 6, 6), (6, 6, 5, 5), (7, 7, 4, 4))
             ]:
                 to_level(1, upper)
         to_partner(1)

time: 40.3 us -> 40 us (level)
  no operation moved by 1% of the time
where the time goes in v6:
time: 40 us; the launch traced here: 39.9 us
  Pallas kernels  39.9 us (100%)
    pallas_call x1, Pallas kernels, on_device(): pl.pallas_call(kernel, out_shape=pltpu.VMEM((N, XB, 128), BF16), in_specs...  39 us
    pallas_call x1, Pallas kernels, on_device(): pl.pallas_call(unpack, out_shape=jax.ShapeDtypeStruct(field_modes.shape,...  0.93 us

profile of v6, /device:TPU:2, one launch (start us, length us, event | category | flops | bytes accessed | tf_op | source)
XLA Modules:
  0.0 39.9 jit_solution(15706478891051095026)
XLA Ops:
  0.0 39.0 %shard_map.55.in_ref = bf16[16,48,128]{2,1,0:T(8,128)(2,1)S(1)} custom-call(bf16[32,4,768]{2,1,0:T(4,128)(2,1)} %fm_hbm.1, bf16[32,4,768]{2,1,0:T(4,128)(2,1)} %ct_hbm.1, bf16[768,768]{1,0:T(8,128)(2,1)} %constant.8.clone.h_hbm, bf16[512,768]{1,0:T(8,128)(2,1)} %constant.6.clone.st_hbm, bf16[512,768]{1,0:T(8,128)(2,1)} %constant.7.clone.pt_hbm), custom_call_target="tpu_custom_call" | custom-call | tf_op jit(solution)/shard_map/pallas_call | solution.py:359
  39.0 0.9 %shard_map.56 = bf16[32,4,768]{2,1,0:T(4,128)(2,1)} custom-call(bf16[16,48,128]{2,1,0:T(8,128)(2,1)S(1)} %shard_map.55.in_ref), custom_call_target="tpu_custom_call" | custom-call | tf_op jit(solution)/shard_map/pallas_call | solution.py:382

commit v7 on v6

--- a/solution.py
+++ b/solution.py
@@ -63,10 +63,14 @@
     x_peer = my_cz + 2 - 4 * (my_cz // 2 % 2)
     y_peers = (lax.rem(my_cz + 4, N), lax.rem(my_cz + 12, N))
     signal(barrier, "kx", partner)
-    signal(barrier, "cz", core_peer)
-    signal(barrier, "cz", x_peer)
-    for peer in y_peers:
-        signal(barrier, "cz", peer)
+
+    @pl.when(level < 4)
+    def _():
+        signal(barrier, "cz", core_peer)
+        signal(barrier, "cz", x_peer)
+        for peer in y_peers:
+            signal(barrier, "cz", peer)
+
     for upper in range(4, 8):
         near = jnp.logical_or(level == upper - 1, level == upper + 1)
 
@@ -88,7 +92,7 @@
     group_ref[...] = (c == (r % 4) * 128 + r // 4).astype(F32).astype(BF16)
     ends = jnp.logical_or(level == 4, level == 7)
     middle = jnp.logical_or(level == 5, level == 6)
-    entered = jnp.where(ends, jnp.where(level == 7, 11, 15), jnp.where(middle, 17, jnp.where(level > 0, 6, 5)))
+    entered = jnp.where(ends, jnp.where(level == 7, 7, 11), jnp.where(middle, 13, jnp.where(level > 0, 6, 5)))
     pl.semaphore_wait(barrier, entered)
 
     @pl.when(level < 3)
@@ -105,8 +109,6 @@
         signal(chain.at[0], "kx", my_kx + 2)
         signal(chain.at[1], "kx", my_kx - 2)
 
-    for peer in y_peers:
-        signal(known.at[0], "cz", peer)
 
     def copy(stage, axis, src, dst, peer):
         return pltpu.make_async_remote_copy(
@@ -256,15 +258,26 @@
     @pl.when(my_cz % 2 == 0)
     def _():
         rest_of_b()
-    pl.semaphore_wait(known.at[0], 2)
-    signal(known.at[1], "cz", x_peer)
-    pl.semaphore_wait(known.at[1], 1)
-    signal(known.at[2], "cz", core_peer)
-    pl.semaphore_wait(known.at[2], 1)
-
-    @pl.when(my_cz % 2 == 1)
-    def _():
-        rest_of_b()
+
+    @pl.when(level < 4)
+    def _():
+        for turn in range(2):
+            for peer in y_peers:
+                signal(known.at[turn], "cz", peer)
+            pl.semaphore_wait(known.at[turn], 2)
+            if turn == 0:
+                @pl.when(my_cz % 2 == 1)
+                def _():
+                    rest_of_b()
+        signal(known.at[2], "cz", x_peer)
+        pl.semaphore_wait(known.at[2], 1)
+        signal(known.at[3], "cz", core_peer)
+        pl.semaphore_wait(known.at[3], 1)
+        for lower, uppers in ((0, (7, 6)), (3, (4, 5))):
+            @pl.when(level == lower)
+            def _():
+                for upper in uppers:
+                    signal(known.at[4], "kx", 2 * upper + side)
 
     def transformed(i, got):
         rows = NX // PARTS
@@ -274,9 +287,17 @@
         if arr == 0:
             loads[2].wait()
         wait_recv(arr, recv1.at[arr])
+        if arr == 0:
+            @pl.when(jnp.logical_and(level >= 4, my_cz % 2 == 1))
+            def _():
+                rest_of_b()
         got = recv1[arr].reshape(NX, 128)
         for i in range(PARTS):
             send2[arr, 8 // PARTS * 2 * i:8 // PARTS * 2 * (i + 1)] = transformed(i, got)
+        if arr == 0:
+            @pl.when(level >= 4)
+            def _():
+                pl.semaphore_wait(known.at[4], 1)
         exchange(2 + arr, "cz", send2.at[arr], recv2.at[arr])
 
     loads[3].wait()
@@ -374,7 +395,7 @@
             pltpu.SemaphoreType.DMA((6,)),
             pltpu.SemaphoreType.DMA((6,)),
             pltpu.SemaphoreType.REGULAR((8,)),
-            pltpu.SemaphoreType.REGULAR((3,)),
+            pltpu.SemaphoreType.REGULAR((5,)),
             pltpu.SemaphoreType.REGULAR((4,)),
         ],
         compiler_params=pltpu.CompilerParams(collective_id=0, has_side_effects=True),

time: 40 us -> 40.2 us (level)
  no operation moved by 1% of the time
where the time goes in v7:
time: 40.2 us; the launch traced here: 40.1 us
  Pallas kernels  40.1 us (100%)
    pallas_call x1, Pallas kernels, on_device(): pl.pallas_call(kernel, out_shape=pltpu.VMEM((N, XB, 128), BF16), in_specs...  39.2 us
    pallas_call x1, Pallas kernels, on_device(): pl.pallas_call(unpack, out_shape=jax.ShapeDtypeStruct(field_modes.shape,...  0.93 us

profile of v7, /device:TPU:2, one launch (start us, length us, event | category | flops | bytes accessed | tf_op | source)
XLA Modules:
  0.0 40.1 jit_solution(8710181019703957857)
XLA Ops:
  0.0 39.2 %shard_map.55.in_ref = bf16[16,48,128]{2,1,0:T(8,128)(2,1)S(1)} custom-call(bf16[32,4,768]{2,1,0:T(4,128)(2,1)} %fm_hbm.1, bf16[32,4,768]{2,1,0:T(4,128)(2,1)} %ct_hbm.1, bf16[768,768]{1,0:T(8,128)(2,1)} %constant.8.clone.h_hbm, bf16[512,768]{1,0:T(8,128)(2,1)} %constant.6.clone.st_hbm, bf16[512,768]{1,0:T(8,128)(2,1)} %constant.7.clone.pt_hbm), custom_call_target="tpu_custom_call" | custom-call | tf_op jit(solution)/shard_map/pallas_call | solution.py:380
  39.2 0.9 %shard_map.56 = bf16[32,4,768]{2,1,0:T(4,128)(2,1)} custom-call(bf16[16,48,128]{2,1,0:T(8,128)(2,1)S(1)} %shard_map.55.in_ref), custom_call_target="tpu_custom_call" | custom-call | tf_op jit(solution)/shard_map/pallas_call | solution.py:403
